TPU v7x, 32 devices: a whole 2x2x4 slice. The times are simulated.
32 devices in a mesh: dp: 8 (over z, x), tensor: 4 (over y, core).
Axes of the slice: x: 2, y: 2, z: 4, core: 2. Of those that a mesh axis runs over, the one named last changes fastest.
Arguments:
- tokens: bfloat16 [32768, 768], P(('dp', 'tensor')), may hold values from -6 to 6
- lengths: int32 [32], P('dp'), may hold values from 256 to 1024, as said below
- w_query: bfloat16 [768, 768], P('dp', 'tensor'), may hold values from -0.3125 to 0.3125
- w_key: bfloat16 [768, 768], P('dp', 'tensor'), may hold values from -0.3125 to 0.3125
- w_value: bfloat16 [768, 768], P('dp', 'tensor'), may hold values from -0.21875 to 0.21875
- w_out: bfloat16 [768, 768], P('tensor', 'dp'), may hold values from -1 to 1
- w_up: bfloat16 [768, 3072], P('dp', 'tensor'), may hold values from -0.21875 to 0.21875
- w_down: bfloat16 [3072, 768], P('tensor', 'dp'), may hold values from -0.109375 to 0.109375
- query_bias: float32 [768], P(('dp', 'tensor')), may hold values from -1.8 to 1.8
- value_bias: float32 [768], P(('dp', 'tensor')), may hold values from -1.8 to 1.8
- out_bias: float32 [768], P(('dp', 'tensor')), may hold values from -1.2 to 1.2
- attn_gain: float32 [768], P(('dp', 'tensor')), may hold values from 0.25 to 1.75
- attn_shift: float32 [768], P(('dp', 'tensor')), may hold values from -1.2 to 1.2
- up_bias: float32 [3072], P(('dp', 'tensor')), may hold values from -1.8 to 1.8
- down_bias: float32 [768], P(('dp', 'tensor')), may hold values from -1.2 to 1.2
- ffn_gain: float32 [768], P(('dp', 'tensor')), may hold values from 0.25 to 1.75
- ffn_shift: float32 [768], P(('dp', 'tensor')), may hold values from -1.8 to 1.8
- cotangent: bfloat16 [32768, 768], P(('dp', 'tensor')), may hold values from -6 to 6
Outputs:
- output: float32 [32768, 768], P(('dp', 'tensor'))
- grad_tokens: float32 [32768, 768], P(('dp', 'tensor'))
- query_grad: float32 [768, 768], P('dp', 'tensor')
- key_grad: float32 [768, 768], P('dp', 'tensor')
- value_grad: float32 [768, 768], P('dp', 'tensor')
- out_grad: float32 [768, 768], P('tensor', 'dp')
- up_grad: float32 [768, 3072], P('dp', 'tensor')
- down_grad: float32 [3072, 768], P('tensor', 'dp')
- query_bias_grad: float32 [768], P(('dp', 'tensor'))
- value_bias_grad: float32 [768], P(('dp', 'tensor'))
- out_bias_grad: float32 [768], P(('dp', 'tensor'))
- attn_gain_grad: float32 [768], P(('dp', 'tensor'))
- attn_shift_grad: float32 [768], P(('dp', 'tensor'))
- up_bias_grad: float32 [3072], P(('dp', 'tensor'))
- down_bias_grad: float32 [768], P(('dp', 'tensor'))
- ffn_gain_grad: float32 [768], P(('dp', 'tensor'))
- ffn_shift_grad: float32 [768], P(('dp', 'tensor'))
Inputs may be any that keep to these rules, and one draw needn't show every extreme that they name: `lengths`: each sequence's count of valid tokens, which come first in it; in every draw some sequence has all 1024 slots valid and some has 256.
All inputs are finite; a program needn't handle non-finite values.
Results may differ from a plain program's by a relative error of at most 0.019.
Values may be sent and summed in bfloat16 or wider, within the bound.
A program may use at most 192 MiB of HBM per device.

v0:
```python
import jax
import jax.numpy as jnp
from jax import lax
from jax.sharding import PartitionSpec as P

HEAD = 64
EPSILON = 1e-12
FLOOR_SCORE = -1e30


def cut_along(shard, dim, peers):
    before, after = (shard.shape[:dim], shard.shape[dim + 1 :])
    return jnp.moveaxis(shard.reshape(*before, peers, -1, *after), dim, 0)


def sum_at_owner(shard, axis, dim):
    parts = cut_along(shard, dim, lax.axis_size(axis))
    arrived = lax.all_to_all(parts, axis, split_axis=0, concat_axis=0, tiled=True)
    return arrived.astype(jnp.float32).sum(axis=0)


def side_by_side(arrays, axis, dim, along):
    widths = [a.shape[along] for a in arrays]
    both = jnp.concatenate(arrays, axis=along)
    whole = sum_at_owner(both, axis, dim)
    return tuple(jnp.split(whole, [sum(widths[:k]) for k in range(1, len(widths))], axis=along))


def matmul(left_side, right_side):
    return jnp.dot(left_side, right_side, preferred_element_type=jnp.float32)


def contract_rows(left_side, right_side):
    return lax.dot_general(
        left_side, right_side, (((0,), (0,)), ((), ())), preferred_element_type=jnp.float32
    )


def contract_cols(left_side, right_side):
    return lax.dot_general(
        left_side, right_side, (((1,), (1,)), ((), ())), preferred_element_type=jnp.float32
    )


def round_trip(operand):
    return lax.optimization_barrier(operand.astype(jnp.bfloat16)).astype(jnp.float32)


def layer_norm(values, norm_gain, norm_shift):
    center = values - jnp.mean(values, axis=-1, keepdims=True)
    spread = jnp.mean(center * center, axis=-1, keepdims=True)
    return center * lax.rsqrt(spread + EPSILON) * norm_gain + norm_shift


def gelu_exact(values):
    return jax.nn.gelu(values, approximate=False)


def head_scores(query_seq, key_seq, length):
    scores = jnp.einsum(
        "qhd,khd->hqk", query_seq, key_seq, preferred_element_type=jnp.float32
    ) * HEAD ** (-0.5)
    counted = jnp.arange(key_seq.shape[0], dtype=jnp.int32) < length
    return (jnp.where(counted[None, None, :], scores, FLOOR_SCORE), counted)


def attend_forward(seq_items):
    query_seq, key_seq, value_seq, length = seq_items
    scores, counted = head_scores(query_seq, key_seq, length)
    row_top = jnp.max(scores, axis=-1, keepdims=True)
    exp_terms = jnp.exp(scores - row_top)
    row_total = jnp.sum(exp_terms, axis=-1, keepdims=True)
    prob_low = (exp_terms / row_total).astype(jnp.bfloat16)
    head_mix = jnp.einsum("hqk,khd->qhd", prob_low, value_seq, preferred_element_type=jnp.float32)
    return (head_mix.astype(jnp.bfloat16), (row_top + jnp.log(row_total))[..., 0])


def attend_backward(seq_items):
    query_seq, key_seq, value_seq, length, log_total, grad_mix = seq_items
    scores, counted = head_scores(query_seq, key_seq, length)
    prob_full = jnp.exp(scores - log_total[..., None])
    prob_low = prob_full.astype(jnp.bfloat16)
    grad_value = jnp.einsum("hqk,qhd->khd", prob_low, grad_mix, preferred_element_type=jnp.float32)
    grad_probs = jnp.einsum("qhd,khd->hqk", grad_mix, value_seq, preferred_element_type=jnp.float32)
    row_inner = jnp.sum(prob_full * grad_probs, axis=-1, keepdims=True)
    grad_scores = jnp.where(
        counted[None, None, :], prob_full * (grad_probs - row_inner), 0.0
    ).astype(jnp.bfloat16)
    score_scale = HEAD ** (-0.5)
    grad_query = (
        jnp.einsum("hqk,khd->qhd", grad_scores, key_seq, preferred_element_type=jnp.float32)
        * score_scale
    )
    grad_key = (
        jnp.einsum("hqk,qhd->khd", grad_scores, query_seq, preferred_element_type=jnp.float32)
        * score_scale
    )
    return (
        grad_query.astype(jnp.bfloat16),
        grad_key.astype(jnp.bfloat16),
        grad_value.astype(jnp.bfloat16),
    )


def shards(
    tokens,
    lengths,
    w_query,
    w_key,
    w_value,
    w_out,
    w_up,
    w_down,
    query_bias,
    value_bias,
    out_bias,
    attn_gain,
    attn_shift,
    up_bias,
    down_bias,
    ffn_gain,
    ffn_shift,
    cotangent,
):
    tensor_rank = lax.axis_index("tensor")
    small_full = (
        lax.all_gather(query_bias, ("dp", "tensor"), axis=0, tiled=True),
        lax.all_gather(value_bias, ("dp", "tensor"), axis=0, tiled=True),
        lax.all_gather(out_bias, ("dp", "tensor"), axis=0, tiled=True),
        lax.all_gather(attn_gain, ("dp", "tensor"), axis=0, tiled=True),
        lax.all_gather(attn_shift, ("dp", "tensor"), axis=0, tiled=True),
        lax.all_gather(up_bias, ("dp", "tensor"), axis=0, tiled=True),
        lax.all_gather(down_bias, ("dp", "tensor"), axis=0, tiled=True),
        lax.all_gather(ffn_gain, ("dp", "tensor"), axis=0, tiled=True),
        lax.all_gather(ffn_shift, ("dp", "tensor"), axis=0, tiled=True),
    )
    (
        qbias_full,
        vbias_full,
        obias_full,
        gain_one,
        shift_one,
        ubias_full,
        dbias_full,
        gain_two,
        shift_two,
    ) = small_full
    query_weight, key_weight, value_weight, out_weight, up_weight, down_weight = (
        lax.all_gather(w_query, "dp", axis=0, tiled=True),
        lax.all_gather(w_key, "dp", axis=0, tiled=True),
        lax.all_gather(w_value, "dp", axis=0, tiled=True),
        lax.all_gather(w_out, "dp", axis=1, tiled=True),
        lax.all_gather(w_up, "dp", axis=0, tiled=True),
        lax.all_gather(w_down, "dp", axis=1, tiled=True),
    )
    row_count = tokens.shape[0]
    model_width = tokens.shape[1]
    head_cols = query_weight.shape[1]
    local_heads = head_cols // HEAD
    seq_count = lengths.shape[0]
    group_total = row_count * lax.axis_size("tensor")
    seq_len = group_total // seq_count
    head_offset = tensor_rank * head_cols

    def to_heads(matrix):
        return matrix.reshape(seq_count, seq_len, local_heads, HEAD)

    group_rows = lax.all_gather(tokens, "tensor", axis=0, tiled=True)
    query_shift = lax.dynamic_slice_in_dim(qbias_full, head_offset, head_cols)
    value_shift = lax.dynamic_slice_in_dim(vbias_full, head_offset, head_cols)
    queries = (matmul(group_rows, query_weight) + query_shift).astype(jnp.bfloat16)
    keys_low = matmul(group_rows, key_weight).astype(jnp.bfloat16)
    values_low = (matmul(group_rows, value_weight) + value_shift).astype(jnp.bfloat16)
    head_mix, log_totals = lax.map(
        attend_forward, (to_heads(queries), to_heads(keys_low), to_heads(values_low), lengths)
    )
    mixed_rows = head_mix.reshape(group_total, head_cols)
    attention = (
        lax.psum_scatter(
            matmul(mixed_rows, out_weight).astype(jnp.bfloat16),
            "tensor",
            scatter_dimension=0,
            tiled=True,
        ).astype(jnp.float32)
        + obias_full
    )
    residual_one = tokens.astype(jnp.float32) + attention
    hidden, norm_one_back = jax.vjp(layer_norm, residual_one, gain_one, shift_one)
    hidden_low = hidden.astype(jnp.bfloat16)
    unit_cols = up_weight.shape[1]
    ffn_rows = lax.all_gather(hidden_low, "tensor", axis=0, tiled=True)
    up_shift = lax.dynamic_slice_in_dim(ubias_full, tensor_rank * unit_cols, unit_cols)
    pre_act = matmul(ffn_rows, up_weight) + up_shift
    act_full, gelu_back = jax.vjp(gelu_exact, pre_act)
    act_low = act_full.astype(jnp.bfloat16)
    branch = (
        lax.psum_scatter(
            matmul(act_low, down_weight).astype(jnp.bfloat16),
            "tensor",
            scatter_dimension=0,
            tiled=True,
        ).astype(jnp.float32)
        + dbias_full
    )
    residual_two = hidden + branch
    normed, norm_two_back = jax.vjp(layer_norm, residual_two, gain_two, shift_two)
    positions = tensor_rank * row_count + jnp.arange(row_count, dtype=jnp.int32)
    seq_of_row = positions // seq_len
    row_length = jnp.sum(
        jnp.where(
            seq_of_row[:, None] == jnp.arange(seq_count, dtype=jnp.int32)[None, :],
            lengths[None, :],
            0,
        ),
        axis=1,
    )
    valid = (positions % seq_len < row_length).astype(jnp.float32)[:, None]
    output = normed * valid
    grad_second, ffn_gain_grad, ffn_shift_grad = norm_two_back(
        cotangent.astype(jnp.float32) * valid
    )
    grad_branch = grad_second.astype(jnp.bfloat16)
    down_bias_grad = jnp.sum(grad_branch.astype(jnp.float32), axis=0)
    branch_rows = lax.all_gather(grad_branch, "tensor", axis=0, tiled=True)
    grad_act = contract_cols(branch_rows, down_weight).astype(jnp.bfloat16)
    down_grad = contract_rows(act_low, branch_rows)
    grad_pre = gelu_back(grad_act.astype(jnp.float32))[0].astype(jnp.bfloat16)
    up_grad = contract_rows(ffn_rows, grad_pre)
    up_part = jnp.sum(grad_pre.astype(jnp.float32), axis=0)
    up_bias_grad = lax.dynamic_update_slice_in_dim(
        jnp.zeros(ubias_full.shape, jnp.float32), up_part, tensor_rank * unit_cols, 0
    )
    grad_from_ffn = lax.psum_scatter(
        contract_cols(grad_pre, up_weight).astype(jnp.bfloat16),
        "tensor",
        scatter_dimension=0,
        tiled=True,
    ).astype(jnp.float32)
    grad_hidden = grad_second + round_trip(grad_from_ffn)
    grad_first, attn_gain_grad, attn_shift_grad = norm_one_back(grad_hidden)
    grad_attn = grad_first.astype(jnp.bfloat16)
    out_bias_grad = jnp.sum(grad_attn.astype(jnp.float32), axis=0)
    attn_grad_rows = lax.all_gather(grad_attn, "tensor", axis=0, tiled=True)
    grad_mixed = contract_cols(attn_grad_rows, out_weight).astype(jnp.bfloat16)
    out_grad = contract_rows(mixed_rows, attn_grad_rows)
    grad_queries, grad_keys, grad_values = lax.map(
        attend_backward,
        (
            to_heads(queries),
            to_heads(keys_low),
            to_heads(values_low),
            lengths,
            log_totals,
            to_heads(grad_mixed),
        ),
    )
    grad_queries = grad_queries.reshape(group_total, head_cols)
    grad_keys = grad_keys.reshape(group_total, head_cols)
    grad_values = grad_values.reshape(group_total, head_cols)
    query_grad = contract_rows(group_rows, grad_queries)
    key_grad = contract_rows(group_rows, grad_keys)
    value_grad = contract_rows(group_rows, grad_values)
    blank_width = jnp.zeros((model_width,), jnp.float32)
    query_bias_grad = lax.dynamic_update_slice_in_dim(
        blank_width, jnp.sum(grad_queries.astype(jnp.float32), axis=0), head_offset, 0
    )
    value_bias_grad = lax.dynamic_update_slice_in_dim(
        blank_width, jnp.sum(grad_values.astype(jnp.float32), axis=0), head_offset, 0
    )
    input_part = (
        contract_cols(grad_queries, query_weight)
        + contract_cols(grad_keys, key_weight)
        + contract_cols(grad_values, value_weight)
    )
    grad_tokens = grad_first + lax.psum_scatter(
        input_part.astype(jnp.bfloat16), "tensor", scatter_dimension=0, tiled=True
    ).astype(jnp.float32)
    owned = (
        *side_by_side(
            (
                query_grad.astype(jnp.bfloat16),
                key_grad.astype(jnp.bfloat16),
                value_grad.astype(jnp.bfloat16),
            ),
            "dp",
            0,
            1,
        ),
        sum_at_owner(out_grad.astype(jnp.bfloat16), "dp", 1),
        sum_at_owner(up_grad.astype(jnp.bfloat16), "dp", 0),
        sum_at_owner(down_grad.astype(jnp.bfloat16), "dp", 1),
    )
    small_owned = (
        lax.psum_scatter(query_bias_grad, ("dp", "tensor"), scatter_dimension=0, tiled=True),
        lax.psum_scatter(value_bias_grad, ("dp", "tensor"), scatter_dimension=0, tiled=True),
        lax.psum_scatter(out_bias_grad, ("dp", "tensor"), scatter_dimension=0, tiled=True),
        lax.psum_scatter(attn_gain_grad, ("dp", "tensor"), scatter_dimension=0, tiled=True),
        lax.psum_scatter(attn_shift_grad, ("dp", "tensor"), scatter_dimension=0, tiled=True),
        lax.psum_scatter(up_bias_grad, ("dp", "tensor"), scatter_dimension=0, tiled=True),
        lax.psum_scatter(down_bias_grad, ("dp", "tensor"), scatter_dimension=0, tiled=True),
        lax.psum_scatter(ffn_gain_grad, ("dp", "tensor"), scatter_dimension=0, tiled=True),
        lax.psum_scatter(ffn_shift_grad, ("dp", "tensor"), scatter_dimension=0, tiled=True),
    )
    return (
        output,
        grad_tokens,
        owned[0],
        owned[1],
        owned[2],
        owned[3],
        owned[4],
        owned[5],
        small_owned[0],
        small_owned[1],
        small_owned[2],
        small_owned[3],
        small_owned[4],
        small_owned[5],
        small_owned[6],
        small_owned[7],
        small_owned[8],
    )


def solution(mesh):
    placed = (
        P(("dp", "tensor"), None),
        P("dp"),
        P("dp", "tensor"),
        P("dp", "tensor"),
        P("dp", "tensor"),
        P("tensor", "dp"),
        P("dp", "tensor"),
        P("tensor", "dp"),
        P(("dp", "tensor")),
        P(("dp", "tensor")),
        P(("dp", "tensor")),
        P(("dp", "tensor")),
        P(("dp", "tensor")),
        P(("dp", "tensor")),
        P(("dp", "tensor")),
        P(("dp", "tensor")),
        P(("dp", "tensor")),
        P(("dp", "tensor"), None),
    )
    return jax.shard_map(
        shards,
        mesh=mesh,
        in_specs=placed,
        out_specs=(
            P(("dp", "tensor"), None),
            P(("dp", "tensor"), None),
            P("dp", "tensor"),
            P("dp", "tensor"),
            P("dp", "tensor"),
            P("tensor", "dp"),
            P("dp", "tensor"),
            P("tensor", "dp"),
            P(("dp", "tensor")),
            P(("dp", "tensor")),
            P(("dp", "tensor")),
            P(("dp", "tensor")),
            P(("dp", "tensor")),
            P(("dp", "tensor")),
            P(("dp", "tensor")),
            P(("dp", "tensor")),
            P(("dp", "tensor")),
        ),
        check_vma=False,
    )
```

profile of v0, /device:TPU:0, one launch (start us, length us, event | category | flops | bytes accessed | tf_op | source)
XLA Modules:
  0.0 1138.1 jit_solution(15248481869915932841)
XLA Ops:
  15.5 44.0 %all-reduce.19 = (f32[768]{0:T(1024)}, f32[768]{0:T(1024)}, f32[768]{0:T(1024)S(1)}, f32[768]{0:T(1024)S(1)}, f32[768]{0:T(1024)S(1)}, /*index=5*/f32[3072]{0:T(1024)}, f32[768]{0:T(1024)}, f32[768]{0:T(1024)}) all-reduce(f32[768]{0:T(1024)S(1)} %dynamic-update-slice.4, ...), channel_id=1, replica_groups=mesh['dp'=8,'tensor'=4] {'dp','tensor'}, use_global_device_ids=true, to_apply=%add.4 | all-reduce | flops 8448 | bytes 67584
  60.6 31.0 %all_gather.63 = bf16[192,768]{0,1:T(8,128)(2,1)S(1)} all-gather(bf16[192,96]{0,1:T(8,128)(2,1)S(1)} %copy.88), channel_id=1, replica_groups=mesh['dp'=8,'tensor'=4] {'dp'}, dimensions={1}, use_global_device_ids=true | all-gather | bytes 331776 | tf_op jit(solution)/shard_map/all_gather | solution.py:152
  91.5 33.2 %all_gather.60 = bf16[768,192]{1,0:T(8,128)(2,1)} all-gather(bf16[96,192]{1,0:T(8,128)(2,1)} %param.24), channel_id=1, replica_groups=mesh['dp'=8,'tensor'=4] {'dp'}, dimensions={0}, use_global_device_ids=true | all-gather | bytes 331776 | tf_op jit(solution)/shard_map/all_gather | solution.py:149
  124.7 33.3 %all_gather.62 = bf16[768,192]{1,0:T(8,128)(2,1)} all-gather(bf16[96,192]{1,0:T(8,128)(2,1)} %param.25), channel_id=1, replica_groups=mesh['dp'=8,'tensor'=4] {'dp'}, dimensions={0}, use_global_device_ids=true | all-gather | bytes 331776 | tf_op jit(solution)/shard_map/all_gather | solution.py:150
  158.0 31.2 %all_gather.58 = bf16[768,192]{1,0:T(8,128)(2,1)S(1)} all-gather(bf16[96,192]{1,0:T(8,128)(2,1)S(1)} %copy-done.42), channel_id=1, replica_groups=mesh['dp'=8,'tensor'=4] {'dp'}, dimensions={0}, use_global_device_ids=true | all-gather | bytes 331776 | tf_op jit(solution)/shard_map/all_gather | solution.py:151
  190.0 5.0 fusion.128
  197.8 5.0 fusion.129
  205.0 5.0 convolution_convert_fusion.5
  215.6 49.6 %while.26 = (s32[]{:T(128)}, bf16[4,1024,3,64]{1,3,2,0:T(8,128)(2,1)}, f32[4,3,1024]{2,1,0:T(4,128)}, bf16[4,1024,3,64]{1,3,2,0:T(8,128)(2,1)}, s32[4]{0:T(128)S...) while((s32[]{:T(128)}, ...), condition=%wide.region_3.4_spmd, body=%wide.region_0.3_spmd.sunk | while | flops 843249664 | bytes 39430256 | solution.py:174
  222.6 4.9 fusion.214
  234.9 4.9 fusion.214
  276.3 58.1 %reduce-scatter.5.cloned.1.call-done = bf16[1024,768]{1,0:T(8,128)(2,1)} async-done(((bf16[4096,768]{1,0:T(8,128)(2,1)}), bf16[1024,768]{1,0:T(8,128)(2,1)}) %reduce-scatter.5.cloned.1.call-update) | async-done | bytes 1572880 | tf_op jit(solution)/shard_map/reduce_scatter | solution.py:179
  340.9 44.9 %all-gather.9.cloned.1.call-done = bf16[4096,768]{1,0:T(8,128)(2,1)} async-done(((bf16[1024,768]{1,0:T(8,128)(2,1)}), bf16[4096,768]{1,0:T(8,128)(2,1)}) %all-gather.9.cloned.1.call-update) | async-done | bytes 6291472 | tf_op jit(solution)/shard_map/all_gather | solution.py:191
  385.9 34.8 %multiply_convert_fusion = (bf16[4096,768]{1,0:T(8,128)(2,1)}, f32[4096,768]{1,0:T(8,128)}, f32[4096,768]{1,0:T(8,128)}) fusion(f32[768]{0:T(1024)S(1)} %dynamic_slice.44, bf16[4096,768]{1,0:T(8,128)(2,1)} %all-gather.9.cloned.1.call-done, bf16[768,768]{1,0:T(8,128)(2,1)} %all-gather.11.cloned.1.call-done), kind=kOutput, calls=%fused_computation.97 | convolution fusion | flops 5039456256 | bytes 38931456 | tf_op jit(solution)/shard_map/dot_general | solution.py:30
  420.7 8.6 all-gather.13.cloned.1.call-done
  429.3 9.2 convolution_convert_fusion.3
  438.9 56.9 %reduce-scatter.7.cloned.1.call-done = bf16[1024,768]{1,0:T(8,128)(2,1)} async-done(((bf16[4096,768]{1,0:T(8,128)(2,1)}), bf16[1024,768]{1,0:T(8,128)(2,1)}) %reduce-scatter.7.cloned.1.call-update) | async-done | bytes 1572880 | tf_op jit(solution)/shard_map/reduce_scatter | solution.py:197
  509.1 46.5 %all-gather.15.cloned.1.call-done = bf16[4096,768]{1,0:T(8,128)(2,1)} async-done(((bf16[1024,768]{1,0:T(8,128)(2,1)}), bf16[4096,768]{1,0:T(8,128)(2,1)}) %all-gather.15.cloned.1.call-update) | async-done | bytes 6291472 | tf_op jit(solution)/shard_map/all_gather | solution.py:224
  555.6 19.1 %convert_reduce_fusion = (f32[768]{0:T(1024)}, bf16[4096,768]{1,0:T(8,128)(2,1)}) fusion(f32[4096,768]{1,0:T(8,128)} %get-tuple-element.253, f32[4096,768]{1,0:T(8,128)} %get-tuple-element.259, f32[768]{0:T(1024)S(1)} %dynamic_slice.44, bf16[4096,768]{1,0:T(8,128)(2,1)} %all-gather.15.cloned.1.call-done, bf16[768,768]{0,1:T(8,128)(2,1)} %all-gather.13.cloned.1.call-done), kind=kOutput, calls=%fused_computation.95 | convolution fusion | flops 4891606016 | bytes 38934528 | tf_op jit(solution)/shard_map/dot_general | solution.py:40
  574.6 9.7 convolution_convert_fusion.1
  584.4 58.8 %reduce-scatter.9.cloned.1.call-done = bf16[1024,768]{1,0:T(8,128)(2,1)} async-done(((bf16[4096,768]{1,0:T(8,128)(2,1)}), bf16[1024,768]{1,0:T(8,128)(2,1)}) %reduce-scatter.9.cloned.1.call-update) | async-done | bytes 1572880 | tf_op jit(solution)/shard_map/reduce_scatter | solution.py:233
  653.9 46.5 %all-gather.17.cloned.1.call-done = bf16[4096,768]{1,0:T(8,128)(2,1)} async-done(((bf16[1024,768]{1,0:T(8,128)(2,1)}), bf16[4096,768]{1,0:T(8,128)(2,1)}) %all-gather.17.cloned.1.call-update) | async-done | bytes 6291472 | tf_op jit(solution)/shard_map/all_gather | solution.py:243
  700.4 5.0 convolution_convert_fusion.4
  712.4 220.9 %while.27 = (s32[]{:T(128)}, bf16[4,1024,3,64]{1,3,2,0:T(8,128)(2,1)}, bf16[4,1024,3,64]{1,3,2,0:T(8,128)(2,1)}, bf16[4,1024,3,64]{1,3,2,0:T(8,128)(2,1)}, bf16[...) while((s32[]{:T(128)}, ...), condition=%wide.region_18.19_spmd, body=%wide.region_16.18_spmd.sunk | while | flops 2096047104 | bytes 199085264 | solution.py:246
  721.3 7.3 fusion.225
  728.6 19.8 %fusion.228 = bf16[4,1024,3,64]{1,3,2,0:T(8,128)(2,1)} fusion(bf16[4,1024,3,64]{1,3,2,0:T(8,128)(2,1)} %get-tuple-element.407, s32[]{:T(128)S(6)} %copy.135, f32[3,1024,1024]{1,2,0:T(8,128)} %fusion.225, f32[3,1024,1024]{1,2,0:T(8,128)} %copy-done, f32[3,1024]{1,0:T(4,128)S(1)} %dynamic-slice_bitcast_fusion.2, ...), kind=kOutput, calls=%fused_computation.52.clone.1 | convolution fusion | flops 437653504 | bytes 51153920 | tf_op jit(solution)/shard_map/while/body/eval_jaxpr/hqk,qhd->khd/dot_general | solution.py:95
  748.4 19.5 %fusion.227 = bf16[4,1024,3,64]{1,3,2,0:T(8,128)(2,1)} fusion(bf16[4,1024,3,64]{1,3,2,0:T(8,128)(2,1)} %get-tuple-element.406, s32[]{:T(128)S(6)} %copy.135, f32[3,1024,1024]{1,2,0:T(8,128)} %fusion.225, f32[3,1024,1024]{1,2,0:T(8,128)} %copy-done, f32[3,1024]{1,0:T(4,128)S(1)} %dynamic-slice_bitcast_fusion.2, ...), kind=kOutput, calls=%fused_computation.50.clone.1 | convolution fusion | flops 437653504 | bytes 51153920 | tf_op jit(solution)/shard_map/while/body/eval_jaxpr/hqk,khd->qhd/dot_general | solution.py:91
  776.4 7.3 fusion.225
  783.7 19.8 %fusion.228 = bf16[4,1024,3,64]{1,3,2,0:T(8,128)(2,1)} fusion(bf16[4,1024,3,64]{1,3,2,0:T(8,128)(2,1)} %get-tuple-element.407, s32[]{:T(128)S(6)} %copy.135, f32[3,1024,1024]{1,2,0:T(8,128)} %fusion.225, f32[3,1024,1024]{1,2,0:T(8,128)} %copy-done, f32[3,1024]{1,0:T(4,128)S(1)} %dynamic-slice_bitcast_fusion.2, ...), kind=kOutput, calls=%fused_computation.52.clone.1 | convolution fusion | flops 437653504 | bytes 51153920 | tf_op jit(solution)/shard_map/while/body/eval_jaxpr/hqk,qhd->khd/dot_general | solution.py:95
  803.5 19.5 %fusion.227 = bf16[4,1024,3,64]{1,3,2,0:T(8,128)(2,1)} fusion(bf16[4,1024,3,64]{1,3,2,0:T(8,128)(2,1)} %get-tuple-element.406, s32[]{:T(128)S(6)} %copy.135, f32[3,1024,1024]{1,2,0:T(8,128)} %fusion.225, f32[3,1024,1024]{1,2,0:T(8,128)} %copy-done, f32[3,1024]{1,0:T(4,128)S(1)} %dynamic-slice_bitcast_fusion.2, ...), kind=kOutput, calls=%fused_computation.50.clone.1 | convolution fusion | flops 437653504 | bytes 51153920 | tf_op jit(solution)/shard_map/while/body/eval_jaxpr/hqk,khd->qhd/dot_general | solution.py:91
  831.4 7.3 fusion.225
  838.8 19.8 %fusion.228 = bf16[4,1024,3,64]{1,3,2,0:T(8,128)(2,1)} fusion(bf16[4,1024,3,64]{1,3,2,0:T(8,128)(2,1)} %get-tuple-element.407, s32[]{:T(128)S(6)} %copy.135, f32[3,1024,1024]{1,2,0:T(8,128)} %fusion.225, f32[3,1024,1024]{1,2,0:T(8,128)} %copy-done, f32[3,1024]{1,0:T(4,128)S(1)} %dynamic-slice_bitcast_fusion.2, ...), kind=kOutput, calls=%fused_computation.52.clone.1 | convolution fusion | flops 437653504 | bytes 51153920 | tf_op jit(solution)/shard_map/while/body/eval_jaxpr/hqk,qhd->khd/dot_general | solution.py:95
  858.6 19.5 %fusion.227 = bf16[4,1024,3,64]{1,3,2,0:T(8,128)(2,1)} fusion(bf16[4,1024,3,64]{1,3,2,0:T(8,128)(2,1)} %get-tuple-element.406, s32[]{:T(128)S(6)} %copy.135, f32[3,1024,1024]{1,2,0:T(8,128)} %fusion.225, f32[3,1024,1024]{1,2,0:T(8,128)} %copy-done, f32[3,1024]{1,0:T(4,128)S(1)} %dynamic-slice_bitcast_fusion.2, ...), kind=kOutput, calls=%fused_computation.50.clone.1 | convolution fusion | flops 437653504 | bytes 51153920 | tf_op jit(solution)/shard_map/while/body/eval_jaxpr/hqk,khd->qhd/dot_general | solution.py:91
  886.6 7.3 fusion.225
  893.9 19.8 %fusion.228 = bf16[4,1024,3,64]{1,3,2,0:T(8,128)(2,1)} fusion(bf16[4,1024,3,64]{1,3,2,0:T(8,128)(2,1)} %get-tuple-element.407, s32[]{:T(128)S(6)} %copy.135, f32[3,1024,1024]{1,2,0:T(8,128)} %fusion.225, f32[3,1024,1024]{1,2,0:T(8,128)} %copy-done, f32[3,1024]{1,0:T(4,128)S(1)} %dynamic-slice_bitcast_fusion.2, ...), kind=kOutput, calls=%fused_computation.52.clone.1 | convolution fusion | flops 437653504 | bytes 51153920 | tf_op jit(solution)/shard_map/while/body/eval_jaxpr/hqk,qhd->khd/dot_general | solution.py:95
  913.7 19.5 %fusion.227 = bf16[4,1024,3,64]{1,3,2,0:T(8,128)(2,1)} fusion(bf16[4,1024,3,64]{1,3,2,0:T(8,128)(2,1)} %get-tuple-element.406, s32[]{:T(128)S(6)} %copy.135, f32[3,1024,1024]{1,2,0:T(8,128)} %fusion.225, f32[3,1024,1024]{1,2,0:T(8,128)} %copy-done, f32[3,1024]{1,0:T(4,128)S(1)} %dynamic-slice_bitcast_fusion.2, ...), kind=kOutput, calls=%fused_computation.50.clone.1 | convolution fusion | flops 437653504 | bytes 51153920 | tf_op jit(solution)/shard_map/while/body/eval_jaxpr/hqk,khd->qhd/dot_general | solution.py:91
  942.5 6.4 fusion.155
  948.9 6.4 fusion.154
  955.3 12.1 %add_convert_fusion = bf16[4096,768]{1,0:T(8,128)(2,1)} fusion(f32[4096,768]{1,0:T(8,128)} %fusion.154, f32[4096,768]{1,0:T(8,128)} %fusion.155, bf16[4096,192]{0,1:T(8,128)(2,1)S(1)} %bitcast.183, bf16[768,192]{1,0:T(8,128)(2,1)S(1)} %copy-done.28), kind=kOutput, calls=%fused_computation.96 | convolution fusion | flops 1217396736 | bytes 33325056 | tf_op jit(solution)/shard_map/dot_general | solution.py:40
  967.4 10.1 convolution_convert_fusion.6
  977.5 5.5 all-to-all-start.3
  983.0 9.8 convolution_convert_fusion.7
  992.9 19.1 %all-to-all-done.3 = bf16[8,768,96]{1,2,0:T(8,128)(2,1)S(1)} async-done(((bf16[8,768,96]{1,2,0:T(8,128)(2,1)}), bf16[8,768,96]{1,2,0:T(8,128)(2,1)S(1)}, u32[]{:S(2)}, u32[]{:S(2)}) %all-to-all-start.3) | async-done | bytes 1179680 | tf_op jit(solution)/shard_map/all_to_all | solution.py:18
  1016.7 5.6 convolution_convert_fusion.8
  1026.5 5.5 fusion.137
  1034.1 11.3 all-to-all-done.2
  1055.2 5.7 all-to-all-done.1
  1074.5 41.1 %all-reduce.18 = (f32[768]{0:T(1024)S(1)}, f32[768]{0:T(1024)S(1)}, f32[768]{0:T(1024)S(1)}, f32[768]{0:T(1024)S(1)}, f32[768]{0:T(1024)S(1)}, /*index=5*/f32[76...) all-reduce(f32[768]{0:T(1024)S(1)} %dynamic-update-slice.8, ...), channel_id=1, replica_groups=mesh['dp'=8,'tensor'=4] {'dp','tensor'}, use_global_device_ids=true, to_apply=%add.8 | all-reduce | flops 9984 | bytes 79872
  (305 shorter events, 200.0 us)
Async XLA Ops:
  8.0 150.0 %copy-start.42 = (bf16[96,192]{1,0:T(8,128)(2,1)S(1)}, bf16[96,192]{1,0:T(8,128)(2,1)}, u32[]{:S(2)}) copy-start(bf16[96,192]{1,0:T(8,128)(2,1)} %param.26) | copy-start | bytes 110596
  8.0 181.2 %all-gather.7.cloned.1.call-start = ((), (), s32[]{:S(2)}) async-start(), calls=%async_computation.8 | async-start | bytes 7864320 | tf_op jit(solution)/shard_map/all_gather | solution.py:168
  8.8 325.7 %reduce-scatter.5.cloned.1.call-start = ((), (), s32[]{:S(2)}) async-start(), calls=%async_computation.9 | async-start | bytes 7864320 | tf_op jit(solution)/shard_map/reduce_scatter | solution.py:179
  91.5 178.1 %copy-start.23 = (bf16[192,768]{0,1:T(8,128)(2,1)}, bf16[192,768]{0,1:T(8,128)(2,1)S(1)}, u32[]{:S(2)}) copy-start(bf16[192,768]{0,1:T(8,128)(2,1)S(1)} %all_gather.63) | copy-start | bytes 884740
  275.3 59.2 %copy-start.3 = (bf16[1024,768]{1,0:T(8,128)(2,1)S(1)}, bf16[1024,768]{1,0:T(8,128)(2,1)}, u32[]{:S(2)}) copy-start(bf16[1024,768]{1,0:T(8,128)(2,1)} %param.22) | copy-start | bytes 4718596
  275.3 65.6 %all-gather.11.cloned.1.call-start = ((), (), s32[]{:S(2)}) async-start(), calls=%async_computation.11 | async-start | bytes 1327104 | tf_op jit(solution)/shard_map/all_gather | solution.py:153
  275.9 110.0 %all-gather.9.cloned.1.call-start = ((), (), s32[]{:S(2)}) async-start(), calls=%async_computation.10 | async-start | bytes 7864320 | tf_op jit(solution)/shard_map/all_gather | solution.py:191
  339.5 89.8 %all-gather.13.cloned.1.call-start = ((), (), s32[]{:S(2)}) async-start(), calls=%async_computation.12 | async-start | bytes 1327104 | tf_op jit(solution)/shard_map/all_gather | solution.py:154
  340.1 155.7 %reduce-scatter.7.cloned.1.call-start = ((), (), s32[]{:S(2)}) async-start(), calls=%async_computation.13 | async-start | bytes 7864320 | tf_op jit(solution)/shard_map/reduce_scatter | solution.py:197
  438.5 57.3 %copy-start.56 = (f32[768]{0:T(1024)S(1)}, f32[768]{0:T(1024)}, u32[]{:S(2)}) copy-start(f32[768]{0:T(1024)} %get-tuple-element.238) | copy-start | bytes 9220
  438.5 117.0 %all-gather.15.cloned.1.call-start = ((), (), s32[]{:S(2)}) async-start(), calls=%async_computation.14 | async-start | bytes 7864320 | tf_op jit(solution)/shard_map/all_gather | solution.py:224
  438.9 64.6 %copy-start.38 = (f32[1024]{0:T(1024)}, f32[1024]{0:T(1024)S(1)}, u32[]{:S(2)}) copy-start(f32[1024]{0:T(1024)S(1)} %fusion.144) | copy-start | bytes 12292
  498.7 4.8 copy-start.1
  498.7 4.8 copy-start.35
  499.2 6.0 copy-start.40
  509.0 134.2 %reduce-scatter.9.cloned.1.call-start = ((), (), s32[]{:S(2)}) async-start(), calls=%async_computation.15 | async-start | bytes 7864320 | tf_op jit(solution)/shard_map/reduce_scatter | solution.py:233
  555.6 19.1 %copy-start.59 = (bf16[768,768]{1,0:T(8,128)(2,1)S(1)}, bf16[768,768]{1,0:T(8,128)(2,1)}, u32[]{:S(2)}) copy-start(bf16[768,768]{1,0:T(8,128)(2,1)} %all-gather.11.cloned.1.call-done) | copy-start | bytes 3538948
  584.4 63.5 %copy-start.46 = (f32[1024]{0:T(1024)S(1)}, f32[1024]{0:T(1024)}, u32[]{:S(2)}) copy-start(f32[1024]{0:T(1024)} %copy-done.45) | copy-start | bytes 12292
  584.4 116.0 %all-gather.17.cloned.1.call-start = ((), (), s32[]{:S(2)}) async-start(), calls=%async_computation.16 | async-start | bytes 7864320 | tf_op jit(solution)/shard_map/all_gather | solution.py:243
  651.8 48.6 %copy-start.24 = (bf16[192,768]{0,1:T(8,128)(2,1)S(1)}, bf16[192,768]{0,1:T(8,128)(2,1)}, u32[]{:S(2)}) copy-start(bf16[192,768]{0,1:T(8,128)(2,1)} %copy-done.23) | copy-start | bytes 884740
  653.9 472.3 %reduce-scatter.11.cloned.1.call-start = ((), (), s32[]{:S(2)}) async-start(), calls=%async_computation.17 | async-start | bytes 7864320 | tf_op jit(solution)/shard_map/reduce_scatter | solution.py:275
  936.7 5.7 copy-start.15
  938.6 10.3 copy-start.16
  942.4 12.9 %copy-start.18 = (bf16[24,8,4,1024]{3,1,2,0:T(8,128)(2,1)}, bf16[24,8,4,1024]{3,1,2,0:T(8,128)(2,1)S(1)}, u32[]{:S(2)}) copy-start(bf16[24,8,4,1024]{3,1,2,0:T(8,128)(2,1)S(1)} %copy.105) | copy-start | bytes 4718596
  942.4 6.4 copy-start.32
  948.9 6.4 copy-start.28
  977.5 34.5 %all-to-all-start.3 = ((bf16[8,768,96]{1,2,0:T(8,128)(2,1)}), bf16[8,768,96]{1,2,0:T(8,128)(2,1)S(1)}, u32[]{:S(2)}, u32[]{:S(2)}) async-start(bf16[8,768,96]{1,2,0:T(8,128)(2,1)} %bitcast.26), calls=%async_computation.7 | async-start | bytes 2359296 | tf_op jit(solution)/shard_map/all_to_all | solution.py:18
  1013.0 32.4 %all-to-all-start.2 = ((bf16[8,96,768]{2,1,0:T(8,128)(2,1)}), bf16[8,96,768]{2,1,0:T(8,128)(2,1)S(1)}, u32[]{:S(2)}, u32[]{:S(2)}) async-start(bf16[8,96,768]{2,1,0:T(8,128)(2,1)} %bitcast.190), calls=%async_computation.6 | async-start | bytes 2359296 | tf_op jit(solution)/shard_map/all_to_all | solution.py:18
  1016.7 15.3 %slice-start = ((s8[6291456]{0:T(1024)(128)(4,1)}), s8[2097152]{0:T(1024)(128)(4,1)S(1)}, s32[]{:S(2)}) async-start(s8[6291456]{0:T(1024)(128)(4,1)} %bitcast.175), calls=%async_computation.18 | async-start | bytes 4194304
  1024.5 7.4 slice-start.1
  1026.5 5.5 copy-start.17
  1045.4 8.4 copy-start.22
  1045.4 15.5 %all-to-all-start.1 = ((bf16[8,192,96]{2,1,0:T(8,128)(2,1)}), bf16[8,192,96]{2,1,0:T(8,128)(2,1)S(1)}, u32[]{:S(2)}, u32[]{:S(2)}) async-start(bf16[8,192,96]{2,1,0:T(8,128)(2,1)} %bitcast.189), calls=%async_computation.5 | async-start | bytes 786432 | tf_op jit(solution)/shard_map/all_to_all | solution.py:18
  1053.8 12.5 %copy-start.60 = (f32[24]{0:T(128)S(1)}, f32[24]{0:T(128)}, u32[]{:S(2)}) copy-start(f32[24]{0:T(128)} %param.38) | copy-start | bytes 292
  1053.8 12.8 %copy-start.57 = (f32[768]{0:T(1024)S(1)}, f32[768]{0:T(1024)}, u32[]{:S(2)}) copy-start(f32[768]{0:T(1024)} %get-tuple-element.242) | copy-start | bytes 9220
  1061.7 62.3 %all-to-all-start = ((bf16[8,96,576]{2,1,0:T(8,128)(2,1)}), bf16[8,96,576]{2,1,0:T(8,128)(2,1)}, u32[]{:S(2)}, u32[]{:S(2)}) async-start(bf16[8,96,576]{2,1,0:T(8,128)(2,1)} %bitcast.22), calls=%async_computation.4 | async-start | bytes 1966080 | tf_op jit(solution)/shard_map/all_to_all | solution.py:18
  1066.2 8.3 copy-start.49
  1066.2 8.3 copy-start.50
  1066.2 8.3 copy-start.51
  1066.2 8.3 copy-start.52
  1066.2 8.3 copy-start.54
  1066.3 8.3 copy-start.55
  1066.3 54.6 %copy-start.2 = (f32[1024,768]{1,0:T(8,128)S(1)}, f32[1024,768]{1,0:T(8,128)}, u32[]{:S(2)}) copy-start(f32[1024,768]{1,0:T(8,128)} %copy-done.1) | copy-start | bytes 9437188
  1066.3 54.6 %copy-start.36 = (f32[1024]{0:T(1024)S(1)}, f32[1024]{0:T(1024)}, u32[]{:S(2)}) copy-start(f32[1024]{0:T(1024)} %copy-done.35) | copy-start | bytes 12292
  1066.3 54.6 %copy-start.39 = (f32[1024]{0:T(1024)S(1)}, f32[1024]{0:T(1024)}, u32[]{:S(2)}) copy-start(f32[1024]{0:T(1024)} %copy-done.38) | copy-start | bytes 12292
  1066.3 54.6 %copy-start.41 = (f32[1024]{0:T(1024)S(1)}, f32[1024]{0:T(1024)}, u32[]{:S(2)}) copy-start(f32[1024]{0:T(1024)} %copy-done.40) | copy-start | bytes 12292
  1066.3 54.6 %copy-start.48 = (f32[768]{0:T(1024)S(1)}, f32[768]{0:T(1024)}, u32[]{:S(2)}) copy-start(f32[768]{0:T(1024)} %get-tuple-element.239) | copy-start | bytes 9220
  1120.9 5.2 copy-start.44
  (35 other events, 103.9 us)
Sparse Core Ops, SparseCore 0:
  10.4 50.5 all-gather.6
  275.4 58.9 reduce-scatter.4
  509.2 46.3 all-gather.14
  654.0 46.3 all-gather.16
Sparse Core Ops, SparseCore 1:
  278.0 41.5 all-gather.10
  339.6 46.2 all-gather.8
  387.9 41.3 all-gather.12
  438.6 57.1 reduce-scatter.6
  584.5 58.7 reduce-scatter.8
  967.5 58.7 reduce-scatter.10
where the time goes:
time: 1150 us; the launch traced here: 1140 us
  matrix products  402 us (35%)
  waiting for transfers between devices  358 us (31%)
  blocking collectives  214 us (19%)
  local copies, waits for them, and re-layouts  68.9 us (6%)
  other arithmetic  59.7 us (5%)
  starting transfers between devices  18.3 us (2%)
  between operations  16.6 us (1%)
    unnamed x2, blocking collectives  85.1 us
    dot_general x4, matrix products, attend_backward(): jnp.einsum('hqk,qhd->khd', grad_scores, query_seq, preferred_element_type...  79.2 us
    dot_general x4, matrix products, attend_backward(): jnp.einsum('hqk,khd->qhd', grad_scores, key_seq, preferred_element_type=j...  77.8 us
    dot_general x6, matrix products, matmul(): return jnp.dot(left_side, right_side, preferred_element_type=jnp.float32)  63.5 us
    reduce_scatter x1, waiting for transfers between devices, shards(): lax.psum_scatter(contract_cols(grad_pre, up_weight).astype(jnp.bfloat16),...  58.8 us
    dot_general x6, matrix products, contract_cols(): lax.dot_general(left_side, right_side, (((1,), (1,)), ((), ())), preferre...  58.7 us
    reduce_scatter x1, waiting for transfers between devices, shards(): lax.psum_scatter(matmul(mixed_rows, out_weight).astype(jnp.bfloat16), 'te...  58.1 us
    reduce_scatter x1, waiting for transfers between devices, shards(): lax.psum_scatter(matmul(act_low, down_weight).astype(jnp.bfloat16), 'tens...  56.9 us
  transfers between devices with their start and end apart: 14, of which 10 were waited for; matrix products, arithmetic and copies ran while one was open for 10% of the time, Pallas kernels for 0%

commit v1 on v0

--- a/solution.py
+++ b/solution.py
@@ -240,7 +240,27 @@
     grad_first, attn_gain_grad, attn_shift_grad = norm_one_back(grad_hidden)
     grad_attn = grad_first.astype(jnp.bfloat16)
     out_bias_grad = jnp.sum(grad_attn.astype(jnp.float32), axis=0)
-    attn_grad_rows = lax.all_gather(grad_attn, "tensor", axis=0, tiled=True)
+    e_next, opened, tall = (lax.axis_size("tensor"), lax.axis_index("tensor"), grad_attn.shape[0])
+    sides = [(to_i, (to_i + 1) % e_next) for to_i in range(e_next)]
+    runs = [(to_i, (to_i - 1) % e_next) for to_i in range(e_next)]
+    attn_grad_rows = jnp.zeros(
+        (*grad_attn.shape[:0], e_next * tall, *grad_attn.shape[0 + 1 :]), grad_attn.dtype
+    )
+    attn_grad_rows = lax.dynamic_update_slice_in_dim(
+        attn_grad_rows, grad_attn, opened * tall, axis=0
+    )
+    block_last = block_next = grad_attn
+    v_next = e_next // 2
+    for it in range(1, v_next + 1):
+        block_last = lax.ppermute(block_last, "tensor", sides)
+        attn_grad_rows = lax.dynamic_update_slice_in_dim(
+            attn_grad_rows, block_last, (opened - it) % e_next * tall, axis=0
+        )
+        if it < e_next - v_next:
+            block_next = lax.ppermute(block_next, axis_name="tensor", perm=runs)
+            attn_grad_rows = lax.dynamic_update_slice_in_dim(
+                attn_grad_rows, block_next, (opened + it) % e_next * tall, axis=0
+            )
     grad_mixed = contract_cols(attn_grad_rows, out_weight).astype(jnp.bfloat16)
     out_grad = contract_rows(mixed_rows, attn_grad_rows)
     grad_queries, grad_keys, grad_values = lax.map(

time: 1150 us -> 1190 us (1.035)
  matrix products: 402 us -> 433 us
    ppermute x0 -> x3, waiting for transfers between devices: none -> 51.8 us  [the longest x2 51.8 us: shards(): block_last = lax.ppermute(block_last, 'tensor', sides)]
    all_gather x1 -> x0, waiting for transfers between devices: 46.5 us -> none  [shards(): attn_grad_rows = lax.all_gather(grad_attn, 'tensor', axis=0, tiled=True)]
    dot_general x8, matrix products: 16.8 us -> 34.9 us  [head_scores(): jnp.einsum('qhd,khd->hqk', query_seq, key_seq, preferred_element_type=jnp...]
    dot_general x4, matrix products: 18.7 us -> 34.1 us  [attend_backward(): jnp.einsum('hqk,qhd->khd', prob_low, grad_mix, preferred_element_type=jnp...]
    unnamed x157 -> x159, local copies, waits for them, and re-layouts: 25.3 us -> 27.2 us
  transfers between devices with their start and end apart: 14 -> 16, of which waited for: 10 -> 11; matrix products, arithmetic and copies ran while one was open for 10% -> 10% of each run, Pallas kernels for 0% -> 0%
where the time goes in v1:
time: 1190 us; the launch traced here: 1180 us
  matrix products  433 us (36%)
  waiting for transfers between devices  360 us (30%)
  blocking collectives  217 us (18%)
  local copies, waits for them, and re-layouts  72.7 us (6%)
  other arithmetic  58.6 us (5%)
  starting transfers between devices  19.8 us (2%)
  between operations  16.9 us (1%)
    unnamed x2, blocking collectives  88.3 us
    dot_general x4, matrix products, attend_backward(): jnp.einsum('hqk,qhd->khd', grad_scores, query_seq, preferred_element_type...  79.2 us
    dot_general x4, matrix products, attend_backward(): jnp.einsum('hqk,khd->qhd', grad_scores, key_seq, preferred_element_type=j...  77.8 us
    dot_general x6, matrix products, matmul(): return jnp.dot(left_side, right_side, preferred_element_type=jnp.float32)  63.6 us
    reduce_scatter x1, waiting for transfers between devices, shards(): lax.psum_scatter(contract_cols(grad_pre, up_weight).astype(jnp.bfloat16),...  58.6 us
    reduce_scatter x1, waiting for transfers between devices, shards(): lax.psum_scatter(matmul(mixed_rows, out_weight).astype(jnp.bfloat16), 'te...  58.4 us
    reduce_scatter x1, waiting for transfers between devices, shards(): lax.psum_scatter(matmul(act_low, down_weight).astype(jnp.bfloat16), 'tens...  57 us
    dot_general x6, matrix products, contract_cols(): lax.dot_general(left_side, right_side, (((1,), (1,)), ((), ())), preferre...  55.9 us
  transfers between devices with their start and end apart: 16, of which 11 were waited for; matrix products, arithmetic and copies ran while one was open for 10% of the time, Pallas kernels for 0%

profile of v1, /device:TPU:0, one launch (start us, length us, event | category | flops | bytes accessed | tf_op | source)
XLA Modules:
  0.0 1179.0 jit_solution(11814351240911911207)
XLA Ops:
  15.5 44.0 %all-reduce.19 = (f32[768]{0:T(1024)}, f32[768]{0:T(1024)}, f32[768]{0:T(1024)S(1)}, f32[768]{0:T(1024)S(1)}, f32[768]{0:T(1024)S(1)}, /*index=5*/f32[3072]{0:T(1024)}, f32[768]{0:T(1024)}, f32[768]{0:T(1024)}) all-reduce(f32[768]{0:T(1024)S(1)} %dynamic-update-slice.4, ...), channel_id=1, replica_groups=mesh['dp'=8,'tensor'=4] {'dp','tensor'}, use_global_device_ids=true, to_apply=%add.4 | all-reduce | flops 8448 | bytes 67584
  60.6 31.2 %all_gather.55 = bf16[768,192]{1,0:T(8,128)(2,1)S(1)} all-gather(bf16[96,192]{1,0:T(8,128)(2,1)} %param.26), channel_id=1, replica_groups=mesh['dp'=8,'tensor'=4] {'dp'}, dimensions={0}, use_global_device_ids=true | all-gather | bytes 331776 | tf_op jit(solution)/shard_map/all_gather | solution.py:151
  91.8 33.3 %all_gather.57 = bf16[768,192]{1,0:T(8,128)(2,1)} all-gather(bf16[96,192]{1,0:T(8,128)(2,1)} %param.24), channel_id=1, replica_groups=mesh['dp'=8,'tensor'=4] {'dp'}, dimensions={0}, use_global_device_ids=true | all-gather | bytes 331776 | tf_op jit(solution)/shard_map/all_gather | solution.py:149
  125.0 33.2 %all_gather.59 = bf16[768,192]{1,0:T(8,128)(2,1)} all-gather(bf16[96,192]{1,0:T(8,128)(2,1)} %param.25), channel_id=1, replica_groups=mesh['dp'=8,'tensor'=4] {'dp'}, dimensions={0}, use_global_device_ids=true | all-gather | bytes 331776 | tf_op jit(solution)/shard_map/all_gather | solution.py:150
  158.2 31.0 %all_gather.60 = bf16[192,768]{0,1:T(8,128)(2,1)S(1)} all-gather(bf16[192,96]{0,1:T(8,128)(2,1)S(1)} %copy.88), channel_id=1, replica_groups=mesh['dp'=8,'tensor'=4] {'dp'}, dimensions={1}, use_global_device_ids=true | all-gather | bytes 331776 | tf_op jit(solution)/shard_map/all_gather | solution.py:152
  215.0 49.6 %while.26 = (s32[]{:T(128)}, bf16[4,1024,3,64]{1,3,2,0:T(8,128)(2,1)}, f32[4,3,1024]{2,1,0:T(4,128)}, bf16[4,1024,3,64]{1,3,2,0:T(8,128)(2,1)}, s32[4]{0:T(128)S...) while((s32[]{:T(128)}, ...), condition=%wide.region_3.4_spmd, body=%wide.region_0.3_spmd.sunk | while | flops 843249664 | bytes 39430756 | solution.py:174
  275.8 58.4 %reduce-scatter.5.cloned.1.call-done = bf16[1024,768]{1,0:T(8,128)(2,1)} async-done(((bf16[4096,768]{1,0:T(8,128)(2,1)}), bf16[1024,768]{1,0:T(8,128)(2,1)}) %reduce-scatter.5.cloned.1.call-update) | async-done | bytes 1572880 | tf_op jit(solution)/shard_map/reduce_scatter | solution.py:179
  340.7 44.9 %all-gather.8.cloned.1.call-done = bf16[4096,768]{1,0:T(8,128)(2,1)} async-done(((bf16[1024,768]{1,0:T(8,128)(2,1)}), bf16[4096,768]{1,0:T(8,128)(2,1)}) %all-gather.8.cloned.1.call-update) | async-done | bytes 6291472 | tf_op jit(solution)/shard_map/all_gather | solution.py:191
  385.6 34.8 %multiply_convert_fusion = (bf16[4096,768]{1,0:T(8,128)(2,1)}, f32[4096,768]{1,0:T(8,128)}, f32[4096,768]{1,0:T(8,128)}) fusion(f32[768]{0:T(1024)S(1)} %dynamic_slice.44, bf16[4096,768]{1,0:T(8,128)(2,1)} %all-gather.8.cloned.1.call-done, bf16[768,768]{1,0:T(8,128)(2,1)} %all-gather.10.cloned.1.call-done), kind=kOutput, calls=%fused_computation.97 | convolution fusion | flops 5039456256 | bytes 38931456 | tf_op jit(solution)/shard_map/dot_general | solution.py:30
  420.5 8.6 all-gather.12.cloned.1.call-done
  429.1 9.2 convolution_convert_fusion.3
  438.7 57.0 %reduce-scatter.7.cloned.1.call-done = bf16[1024,768]{1,0:T(8,128)(2,1)} async-done(((bf16[4096,768]{1,0:T(8,128)(2,1)}), bf16[1024,768]{1,0:T(8,128)(2,1)}) %reduce-scatter.7.cloned.1.call-update) | async-done | bytes 1572880 | tf_op jit(solution)/shard_map/reduce_scatter | solution.py:197
  508.9 46.5 %all-gather.14.cloned.1.call-done = bf16[4096,768]{1,0:T(8,128)(2,1)} async-done(((bf16[1024,768]{1,0:T(8,128)(2,1)}), bf16[4096,768]{1,0:T(8,128)(2,1)}) %all-gather.14.cloned.1.call-update) | async-done | bytes 6291472 | tf_op jit(solution)/shard_map/all_gather | solution.py:224
  555.4 19.1 %convert_reduce_fusion = (f32[768]{0:T(1024)}, bf16[4096,768]{1,0:T(8,128)(2,1)}) fusion(f32[4096,768]{1,0:T(8,128)} %get-tuple-element.253, f32[4096,768]{1,0:T(8,128)} %get-tuple-element.259, f32[768]{0:T(1024)S(1)} %dynamic_slice.44, bf16[4096,768]{1,0:T(8,128)(2,1)} %all-gather.14.cloned.1.call-done, bf16[768,768]{0,1:T(8,128)(2,1)} %all-gather.12.cloned.1.call-done), kind=kOutput, calls=%fused_computation.95 | convolution fusion | flops 4891606016 | bytes 38934528 | tf_op jit(solution)/shard_map/dot_general | solution.py:40
  574.5 9.7 convolution_convert_fusion.1
  584.5 58.6 %reduce-scatter.9.cloned.1.call-done = bf16[1024,768]{1,0:T(8,128)(2,1)} async-done(((bf16[4096,768]{1,0:T(8,128)(2,1)}), bf16[1024,768]{1,0:T(8,128)(2,1)}) %reduce-scatter.9.cloned.1.call-update) | async-done | bytes 1572880 | tf_op jit(solution)/shard_map/reduce_scatter | solution.py:233
  654.3 34.3 %collective-permute-done = bf16[1024,768]{1,0:T(8,128)(2,1)S(1)} collective-permute-done((bf16[1024,768]{1,0:T(8,128)(2,1)S(1)}, bf16[1024,768]{1,0:T(8,128)(2,1)S(1)}, u32[]{:S(2)}, u32[]{:S(2)}) %collective-permute-start) | collective-permute-done | bytes 1572896 | tf_op jit(solution)/shard_map/ppermute | solution.py:255
  691.0 17.5 %collective-permute-done.2 = bf16[1024,768]{1,0:T(8,128)(2,1)} collective-permute-done((bf16[1024,768]{1,0:T(8,128)(2,1)S(1)}, bf16[1024,768]{1,0:T(8,128)(2,1)}, u32[]{:S(2)}, u32[]{:S(2)}) %collective-permute-start.2) | collective-permute-done | bytes 1572896 | tf_op jit(solution)/shard_map/ppermute | solution.py:255
  722.0 254.8 %while.27 = (s32[]{:T(128)}, bf16[4,1024,3,64]{1,3,2,0:T(8,128)(2,1)}, bf16[4,1024,3,64]{1,3,2,0:T(8,128)(2,1)}, bf16[4,1024,3,64]{1,3,2,0:T(8,128)(2,1)}, bf16[...) while((s32[]{:T(128)}, ...), condition=%wide.region_18.19_spmd, body=%wide.region_16.18_spmd.sunk | while | flops 2096047104 | bytes 142458000 | solution.py:266
  722.3 6.4 fusion.226
  728.7 7.5 fusion.225
  738.1 19.8 %fusion.228 = bf16[4,1024,3,64]{1,3,2,0:T(8,128)(2,1)} fusion(bf16[4,1024,3,64]{1,3,2,0:T(8,128)(2,1)} %get-tuple-element.407, s32[]{:T(128)} %get-tuple-element.405, f32[3,1024,1024]{1,2,0:T(8,128)} %fusion.225, f32[3,1024,1024]{1,2,0:T(8,128)} %fusion.226, f32[3,1024]{1,0:T(4,128)S(1)} %dynamic-slice_bitcast_fusion.2, ...), kind=kOutput, calls=%fused_computation.52.clone.1 | convolution fusion | flops 437653504 | bytes 51153920 | tf_op jit(solution)/shard_map/while/body/eval_jaxpr/hqk,qhd->khd/dot_general | solution.py:95
  757.9 19.5 %fusion.227 = bf16[4,1024,3,64]{1,3,2,0:T(8,128)(2,1)} fusion(bf16[4,1024,3,64]{1,3,2,0:T(8,128)(2,1)} %get-tuple-element.406, s32[]{:T(128)} %get-tuple-element.405, f32[3,1024,1024]{1,2,0:T(8,128)} %fusion.225, f32[3,1024,1024]{1,2,0:T(8,128)} %fusion.226, f32[3,1024]{1,0:T(4,128)S(1)} %dynamic-slice_bitcast_fusion.2, ...), kind=kOutput, calls=%fused_computation.50.clone.1 | convolution fusion | flops 437653504 | bytes 51153920 | tf_op jit(solution)/shard_map/while/body/eval_jaxpr/hqk,khd->qhd/dot_general | solution.py:91
  777.4 8.5 fusion.229
  785.9 6.4 fusion.226
  792.3 7.5 fusion.225
  801.7 19.8 %fusion.228 = bf16[4,1024,3,64]{1,3,2,0:T(8,128)(2,1)} fusion(bf16[4,1024,3,64]{1,3,2,0:T(8,128)(2,1)} %get-tuple-element.407, s32[]{:T(128)} %get-tuple-element.405, f32[3,1024,1024]{1,2,0:T(8,128)} %fusion.225, f32[3,1024,1024]{1,2,0:T(8,128)} %fusion.226, f32[3,1024]{1,0:T(4,128)S(1)} %dynamic-slice_bitcast_fusion.2, ...), kind=kOutput, calls=%fused_computation.52.clone.1 | convolution fusion | flops 437653504 | bytes 51153920 | tf_op jit(solution)/shard_map/while/body/eval_jaxpr/hqk,qhd->khd/dot_general | solution.py:95
  821.5 19.5 %fusion.227 = bf16[4,1024,3,64]{1,3,2,0:T(8,128)(2,1)} fusion(bf16[4,1024,3,64]{1,3,2,0:T(8,128)(2,1)} %get-tuple-element.406, s32[]{:T(128)} %get-tuple-element.405, f32[3,1024,1024]{1,2,0:T(8,128)} %fusion.225, f32[3,1024,1024]{1,2,0:T(8,128)} %fusion.226, f32[3,1024]{1,0:T(4,128)S(1)} %dynamic-slice_bitcast_fusion.2, ...), kind=kOutput, calls=%fused_computation.50.clone.1 | convolution fusion | flops 437653504 | bytes 51153920 | tf_op jit(solution)/shard_map/while/body/eval_jaxpr/hqk,khd->qhd/dot_general | solution.py:91
  840.9 8.5 fusion.229
  849.4 6.4 fusion.226
  855.8 7.5 fusion.225
  865.2 19.8 %fusion.228 = bf16[4,1024,3,64]{1,3,2,0:T(8,128)(2,1)} fusion(bf16[4,1024,3,64]{1,3,2,0:T(8,128)(2,1)} %get-tuple-element.407, s32[]{:T(128)} %get-tuple-element.405, f32[3,1024,1024]{1,2,0:T(8,128)} %fusion.225, f32[3,1024,1024]{1,2,0:T(8,128)} %fusion.226, f32[3,1024]{1,0:T(4,128)S(1)} %dynamic-slice_bitcast_fusion.2, ...), kind=kOutput, calls=%fused_computation.52.clone.1 | convolution fusion | flops 437653504 | bytes 51153920 | tf_op jit(solution)/shard_map/while/body/eval_jaxpr/hqk,qhd->khd/dot_general | solution.py:95
  885.0 19.5 %fusion.227 = bf16[4,1024,3,64]{1,3,2,0:T(8,128)(2,1)} fusion(bf16[4,1024,3,64]{1,3,2,0:T(8,128)(2,1)} %get-tuple-element.406, s32[]{:T(128)} %get-tuple-element.405, f32[3,1024,1024]{1,2,0:T(8,128)} %fusion.225, f32[3,1024,1024]{1,2,0:T(8,128)} %fusion.226, f32[3,1024]{1,0:T(4,128)S(1)} %dynamic-slice_bitcast_fusion.2, ...), kind=kOutput, calls=%fused_computation.50.clone.1 | convolution fusion | flops 437653504 | bytes 51153920 | tf_op jit(solution)/shard_map/while/body/eval_jaxpr/hqk,khd->qhd/dot_general | solution.py:91
  904.5 8.5 fusion.229
  913.0 6.4 fusion.226
  919.4 7.5 fusion.225
  928.8 19.8 %fusion.228 = bf16[4,1024,3,64]{1,3,2,0:T(8,128)(2,1)} fusion(bf16[4,1024,3,64]{1,3,2,0:T(8,128)(2,1)} %get-tuple-element.407, s32[]{:T(128)} %get-tuple-element.405, f32[3,1024,1024]{1,2,0:T(8,128)} %fusion.225, f32[3,1024,1024]{1,2,0:T(8,128)} %fusion.226, f32[3,1024]{1,0:T(4,128)S(1)} %dynamic-slice_bitcast_fusion.2, ...), kind=kOutput, calls=%fused_computation.52.clone.1 | convolution fusion | flops 437653504 | bytes 51153920 | tf_op jit(solution)/shard_map/while/body/eval_jaxpr/hqk,qhd->khd/dot_general | solution.py:95
  948.6 19.5 %fusion.227 = bf16[4,1024,3,64]{1,3,2,0:T(8,128)(2,1)} fusion(bf16[4,1024,3,64]{1,3,2,0:T(8,128)(2,1)} %get-tuple-element.406, s32[]{:T(128)} %get-tuple-element.405, f32[3,1024,1024]{1,2,0:T(8,128)} %fusion.225, f32[3,1024,1024]{1,2,0:T(8,128)} %fusion.226, f32[3,1024]{1,0:T(4,128)S(1)} %dynamic-slice_bitcast_fusion.2, ...), kind=kOutput, calls=%fused_computation.50.clone.1 | convolution fusion | flops 437653504 | bytes 51153920 | tf_op jit(solution)/shard_map/while/body/eval_jaxpr/hqk,khd->qhd/dot_general | solution.py:91
  968.1 8.5 fusion.229
  984.0 6.4 fusion.154
  990.4 6.4 fusion.155
  996.8 12.1 %add_convert_fusion = bf16[4096,768]{1,0:T(8,128)(2,1)} fusion(f32[4096,768]{1,0:T(8,128)} %fusion.154, f32[4096,768]{1,0:T(8,128)} %fusion.155, bf16[4096,192]{0,1:T(8,128)(2,1)S(1)} %bitcast.183, bf16[768,192]{1,0:T(8,128)(2,1)S(1)} %copy-done.28), kind=kOutput, calls=%fused_computation.96 | convolution fusion | flops 1217396736 | bytes 33325056 | tf_op jit(solution)/shard_map/dot_general | solution.py:40
  1009.0 10.1 convolution_convert_fusion.6
  1024.4 9.9 convolution_convert_fusion.7
  1034.3 16.2 %all-to-all-done.3 = bf16[8,768,96]{1,2,0:T(8,128)(2,1)S(1)} async-done(((bf16[8,768,96]{1,2,0:T(8,128)(2,1)}), bf16[8,768,96]{1,2,0:T(8,128)(2,1)S(1)}, u32[]{:S(2)}, u32[]{:S(2)}) %all-to-all-start.3) | async-done | bytes 1179680 | tf_op jit(solution)/shard_map/all_to_all | solution.py:18
  1072.5 10.6 all-to-all-done.2
  1092.8 5.6 all-to-all-done.1
  1112.0 44.3 %all-reduce.18 = (f32[768]{0:T(1024)S(1)}, f32[768]{0:T(1024)S(1)}, f32[768]{0:T(1024)S(1)}, f32[768]{0:T(1024)S(1)}, f32[768]{0:T(1024)S(1)}, /*index=5*/f32[76...) all-reduce(f32[768]{0:T(1024)S(1)} %dynamic-update-slice.8, ...), channel_id=1, replica_groups=mesh['dp'=8,'tensor'=4] {'dp','tensor'}, use_global_device_ids=true, to_apply=%add.8 | all-reduce | flops 9984 | bytes 79872
  (299 shorter events, 221.9 us)
Async XLA Ops:
  8.0 181.2 %all-gather.6.cloned.1.call-start = ((), (), s32[]{:S(2)}) async-start(), calls=%async_computation.8 | async-start | bytes 7864320 | tf_op jit(solution)/shard_map/all_gather | solution.py:168
  8.8 325.5 %reduce-scatter.5.cloned.1.call-start = ((), (), s32[]{:S(2)}) async-start(), calls=%async_computation.9 | async-start | bytes 7864320 | tf_op jit(solution)/shard_map/reduce_scatter | solution.py:179
  91.8 97.5 %copy-start.27 = (bf16[768,192]{1,0:T(8,128)(2,1)}, bf16[768,192]{1,0:T(8,128)(2,1)S(1)}, u32[]{:S(2)}) copy-start(bf16[768,192]{1,0:T(8,128)(2,1)S(1)} %all_gather.55) | copy-start | bytes 884740
  189.2 79.8 %copy-start.23 = (bf16[192,768]{0,1:T(8,128)(2,1)}, bf16[192,768]{0,1:T(8,128)(2,1)S(1)}, u32[]{:S(2)}) copy-start(bf16[192,768]{0,1:T(8,128)(2,1)S(1)} %all_gather.60) | copy-start | bytes 884740
  274.7 59.5 %copy-start.2 = (bf16[1024,768]{1,0:T(8,128)(2,1)S(1)}, bf16[1024,768]{1,0:T(8,128)(2,1)}, u32[]{:S(2)}) copy-start(bf16[1024,768]{1,0:T(8,128)(2,1)} %param.22) | copy-start | bytes 4718596
  274.7 66.0 %all-gather.10.cloned.1.call-start = ((), (), s32[]{:S(2)}) async-start(), calls=%async_computation.11 | async-start | bytes 1327104 | tf_op jit(solution)/shard_map/all_gather | solution.py:153
  275.3 110.3 %all-gather.8.cloned.1.call-start = ((), (), s32[]{:S(2)}) async-start(), calls=%async_computation.10 | async-start | bytes 7864320 | tf_op jit(solution)/shard_map/all_gather | solution.py:191
  339.3 89.8 %all-gather.12.cloned.1.call-start = ((), (), s32[]{:S(2)}) async-start(), calls=%async_computation.12 | async-start | bytes 1327104 | tf_op jit(solution)/shard_map/all_gather | solution.py:154
  339.9 155.7 %reduce-scatter.7.cloned.1.call-start = ((), (), s32[]{:S(2)}) async-start(), calls=%async_computation.13 | async-start | bytes 7864320 | tf_op jit(solution)/shard_map/reduce_scatter | solution.py:197
  438.3 57.4 %copy-start.55 = (f32[768]{0:T(1024)S(1)}, f32[768]{0:T(1024)}, u32[]{:S(2)}) copy-start(f32[768]{0:T(1024)} %get-tuple-element.238) | copy-start | bytes 9220
  438.3 117.1 %all-gather.14.cloned.1.call-start = ((), (), s32[]{:S(2)}) async-start(), calls=%async_computation.14 | async-start | bytes 7864320 | tf_op jit(solution)/shard_map/all_gather | solution.py:224
  438.6 64.7 %copy-start.38 = (f32[1024]{0:T(1024)}, f32[1024]{0:T(1024)S(1)}, u32[]{:S(2)}) copy-start(f32[1024]{0:T(1024)S(1)} %fusion.144) | copy-start | bytes 12292
  499.1 6.0 copy-start.40
  508.9 134.2 %reduce-scatter.9.cloned.1.call-start = ((), (), s32[]{:S(2)}) async-start(), calls=%async_computation.15 | async-start | bytes 7864320 | tf_op jit(solution)/shard_map/reduce_scatter | solution.py:233
  555.4 19.1 %copy-start.58 = (bf16[768,768]{1,0:T(8,128)(2,1)S(1)}, bf16[768,768]{1,0:T(8,128)(2,1)}, u32[]{:S(2)}) copy-start(bf16[768,768]{1,0:T(8,128)(2,1)} %all-gather.10.cloned.1.call-done) | copy-start | bytes 3538948
  584.2 63.5 %copy-start.45 = (f32[1024]{0:T(1024)S(1)}, f32[1024]{0:T(1024)}, u32[]{:S(2)}) copy-start(f32[1024]{0:T(1024)} %copy-done.44) | copy-start | bytes 12292
  584.2 582.5 %reduce-scatter.11.cloned.1.call-start = ((), (), s32[]{:S(2)}) async-start(), calls=%async_computation.16 | async-start | bytes 7864320 | tf_op jit(solution)/shard_map/reduce_scatter | solution.py:295
  649.9 38.7 %copy-start.42 = (f32[1024]{0:T(1024)}, f32[1024]{0:T(1024)S(1)}, u32[]{:S(2)}) copy-start(f32[1024]{0:T(1024)S(1)} %negate_multiply_fusion.1) | copy-start | bytes 12292
  652.5 36.0 %collective-permute-start = (bf16[1024,768]{1,0:T(8,128)(2,1)S(1)}, bf16[1024,768]{1,0:T(8,128)(2,1)S(1)}, u32[]{:S(2)}, u32[]{:S(2)}) collective-permute-start(bf16[1024,768]{1,0:T(8,128)(2,1)S(1)} %get-tuple-element.245), channel_id=1, source_target_pairs={{0,1},{1,2},{2,3},{3,0},{4,5},{5,6},{6,7},{7,4},{8,9},{9,10},{10,1... | collective-permute-start | bytes 4718600 | tf_op jit(solution)/shard_map/ppermute | solution.py:255
  652.5 36.8 %collective-permute-start.1 = (bf16[1024,768]{1,0:T(8,128)(2,1)S(1)}, bf16[1024,768]{1,0:T(8,128)(2,1)}, u32[]{:S(2)}, u32[]{:S(2)}) collective-permute-start(bf16[1024,768]{1,0:T(8,128)(2,1)S(1)} %get-tuple-element.245), channel_id=1, source_target_pairs={{0,3},{1,0},{2,1},{3,2},{4,7},{5,4},{6,5},{7,6},{8,11},{9,8},{10,9... | collective-permute-start | bytes 4718600 | tf_op jit(solution)/shard_map/ppermute | solution.py:260
  688.6 19.9 %collective-permute-start.2 = (bf16[1024,768]{1,0:T(8,128)(2,1)S(1)}, bf16[1024,768]{1,0:T(8,128)(2,1)}, u32[]{:S(2)}, u32[]{:S(2)}) collective-permute-start(bf16[1024,768]{1,0:T(8,128)(2,1)S(1)} %collective-permute-done), channel_id=1, source_target_pairs={{0,1},{1,2},{2,3},{3,0},{4,5},{5,6},{6,7},{7,4},{8,9},{9,10},{10,1... | collective-permute-start | bytes 4718600 | tf_op jit(solution)/shard_map/ppermute | solution.py:255
  689.3 23.3 %copy-start.24 = (bf16[192,768]{0,1:T(8,128)(2,1)S(1)}, bf16[192,768]{0,1:T(8,128)(2,1)}, u32[]{:S(2)}) copy-start(bf16[192,768]{0,1:T(8,128)(2,1)} %copy-done.23) | copy-start | bytes 884740
  982.0 8.4 copy-start.15
  984.0 12.9 %copy-start.17 = (bf16[24,8,4,1024]{3,1,2,0:T(8,128)(2,1)}, bf16[24,8,4,1024]{3,1,2,0:T(8,128)(2,1)S(1)}, u32[]{:S(2)}) copy-start(bf16[24,8,4,1024]{3,1,2,0:T(8,128)(2,1)S(1)} %copy.105) | copy-start | bytes 4718596
  984.0 6.4 copy-start.26
  990.4 6.4 copy-start.28
  1019.1 31.5 %all-to-all-start.3 = ((bf16[8,768,96]{1,2,0:T(8,128)(2,1)}), bf16[8,768,96]{1,2,0:T(8,128)(2,1)S(1)}, u32[]{:S(2)}, u32[]{:S(2)}) async-start(bf16[8,768,96]{1,2,0:T(8,128)(2,1)} %bitcast.26), calls=%async_computation.7 | async-start | bytes 2359296 | tf_op jit(solution)/shard_map/all_to_all | solution.py:18
  1051.6 31.6 %all-to-all-start.2 = ((bf16[8,96,768]{2,1,0:T(8,128)(2,1)}), bf16[8,96,768]{2,1,0:T(8,128)(2,1)S(1)}, u32[]{:S(2)}, u32[]{:S(2)}) async-start(bf16[8,96,768]{2,1,0:T(8,128)(2,1)} %bitcast.190), calls=%async_computation.6 | async-start | bytes 2359296 | tf_op jit(solution)/shard_map/all_to_all | solution.py:18
  1055.1 15.2 %slice-start = ((s8[6291456]{0:T(1024)(128)(4,1)}), s8[2097152]{0:T(1024)(128)(4,1)S(1)}, s32[]{:S(2)}) async-start(s8[6291456]{0:T(1024)(128)(4,1)} %bitcast.175), calls=%async_computation.17 | async-start | bytes 4194304
  1062.8 7.5 slice-start.1
  1064.8 5.6 copy-start.16
  1083.2 8.2 copy-start.22
  1083.2 15.2 %all-to-all-start.1 = ((bf16[8,192,96]{2,1,0:T(8,128)(2,1)}), bf16[8,192,96]{2,1,0:T(8,128)(2,1)S(1)}, u32[]{:S(2)}, u32[]{:S(2)}) async-start(bf16[8,192,96]{2,1,0:T(8,128)(2,1)} %bitcast.189), calls=%async_computation.5 | async-start | bytes 786432 | tf_op jit(solution)/shard_map/all_to_all | solution.py:18
  1091.4 12.4 %copy-start.59 = (f32[24]{0:T(128)S(1)}, f32[24]{0:T(128)}, u32[]{:S(2)}) copy-start(f32[24]{0:T(128)} %param.38) | copy-start | bytes 292
  1091.4 12.7 %copy-start.56 = (f32[768]{0:T(1024)S(1)}, f32[768]{0:T(1024)}, u32[]{:S(2)}) copy-start(f32[768]{0:T(1024)} %get-tuple-element.242) | copy-start | bytes 9220
  1099.2 65.5 %all-to-all-start = ((bf16[8,96,576]{2,1,0:T(8,128)(2,1)}), bf16[8,96,576]{2,1,0:T(8,128)(2,1)}, u32[]{:S(2)}, u32[]{:S(2)}) async-start(bf16[8,96,576]{2,1,0:T(8,128)(2,1)} %bitcast.22), calls=%async_computation.4 | async-start | bytes 1966080 | tf_op jit(solution)/shard_map/all_to_all | solution.py:18
  1103.7 8.3 copy-start.48
  1103.7 8.3 copy-start.49
  1103.7 8.3 copy-start.50
  1103.7 8.3 copy-start.51
  1103.7 8.3 copy-start.53
  1103.7 8.3 copy-start.54
  1103.7 57.8 %copy-start.1 = (f32[1024,768]{1,0:T(8,128)S(1)}, f32[1024,768]{1,0:T(8,128)}, u32[]{:S(2)}) copy-start(f32[1024,768]{1,0:T(8,128)} %copy-done) | copy-start | bytes 9437188
  1103.7 57.8 %copy-start.36 = (f32[1024]{0:T(1024)S(1)}, f32[1024]{0:T(1024)}, u32[]{:S(2)}) copy-start(f32[1024]{0:T(1024)} %copy-done.35) | copy-start | bytes 12292
  1103.7 57.8 %copy-start.39 = (f32[1024]{0:T(1024)S(1)}, f32[1024]{0:T(1024)}, u32[]{:S(2)}) copy-start(f32[1024]{0:T(1024)} %copy-done.38) | copy-start | bytes 12292
  1103.8 57.8 %copy-start.41 = (f32[1024]{0:T(1024)S(1)}, f32[1024]{0:T(1024)}, u32[]{:S(2)}) copy-start(f32[1024]{0:T(1024)} %copy-done.40) | copy-start | bytes 12292
  1103.8 57.8 %copy-start.47 = (f32[768]{0:T(1024)S(1)}, f32[768]{0:T(1024)}, u32[]{:S(2)}) copy-start(f32[768]{0:T(1024)} %get-tuple-element.239) | copy-start | bytes 9220
  1161.6 5.2 copy-start.43
  (30 other events, 89.3 us)
Sparse Core Ops, SparseCore 0:
  10.4 50.5 all-gather.5
  274.9 59.3 reduce-scatter.4
  509.0 46.3 all-gather.13
  1009.1 58.6 reduce-scatter.10
Sparse Core Ops, SparseCore 1:
  277.4 41.8 all-gather.9
  339.4 46.2 all-gather.7
  387.7 41.4 all-gather.11
  438.4 57.2 reduce-scatter.6
  584.3 58.7 reduce-scatter.8
